TPU v7x, 32 devices: a whole 2x2x4 slice. The times are simulated.
32 devices in a mesh: fsdp: 8 (over z, x), grp: 4 (over y, core).
Axes of the slice: x: 2, y: 2, z: 4, core: 2. Of those that a mesh axis runs over, the one named last changes fastest.
Arguments:
- gradient: bfloat16 [24, 512, 512], P('fsdp', 'grp'), may hold values from -6 to 6
- left_factor: bfloat16 [96, 512, 512], P(('fsdp', 'grp'))
- right_factor: bfloat16 [96, 512, 512], P(('fsdp', 'grp'))
- block_owner: int32 [24], replicated, may hold values from 0 to 31, as said below
Outputs:
- preconditioned: bfloat16 [24, 512, 512], P('fsdp', 'grp')
Inputs may be any that keep to these rules, and one draw needn't show every extreme that they name: block_owner[b] is a device index, fsdp index times 4 plus grp index. The 3 blocks homed at one fsdp index go to devices of 3 different fsdp indices; the devices of each fsdp index own 3 blocks in all; no device owns more than 3 blocks, and at every fsdp index one device owns exactly 3.
All inputs are finite; a program needn't handle non-finite values.
Results may differ from a plain program's by a relative error of at most 0.0049.
Values may be sent and summed in bfloat16 or wider, within the bound.
A program may use at most 64 MiB of HBM per device.

v0:
```python
import jax
import jax.numpy as jnp
from jax import lax
from jax.sharding import PartitionSpec as P


def per_device(gradient, left_factor, right_factor, block_owner):
    local_blocks = gradient.shape[0]
    piece_rows = gradient.shape[1]
    block_width = gradient.shape[2]
    slot_count = left_factor.shape[0]
    columns = lax.axis_size("fsdp")
    groups = lax.axis_size("grp")
    column = lax.axis_index("fsdp")
    owners_all = block_owner.reshape(columns, local_blocks)
    dest_column = owners_all // groups
    dest_group = owners_all % groups
    mine_column = lax.dynamic_index_in_dim(dest_column, column, 0, keepdims=False)
    column_ids = jnp.arange(columns, dtype=jnp.int32)
    matching = mine_column[None, :] == column_ids[:, None]
    pick_send = matching.astype(jnp.bfloat16)
    outgoing = jnp.einsum(
        "cj,jrd->crd", pick_send, gradient, preferred_element_type=jnp.float32
    ).astype(jnp.bfloat16)
    arrived = lax.all_to_all(
        outgoing.reshape(columns * piece_rows, block_width),
        "fsdp",
        split_axis=0,
        concat_axis=0,
        tiled=True,
    )
    arrived = arrived.reshape(columns, piece_rows, block_width)
    toward = dest_column == column
    live_source = jnp.sum(toward.astype(jnp.int32), axis=1) > 0
    target = jnp.sum(jnp.where(toward, dest_group, 0), axis=1)
    same_owner = (target[None, :] == target[:, None]) & live_source[None, :] & live_source[:, None]
    before = column_ids[None, :] < column_ids[:, None]
    rank_slot = jnp.sum((same_owner & before).astype(jnp.int32), axis=1)
    group_ids = jnp.arange(groups, dtype=jnp.int32)
    slot_ids = jnp.arange(slot_count, dtype=jnp.int32)
    routing = (
        live_source[None, None, :]
        & (target[None, None, :] == group_ids[:, None, None])
        & (rank_slot[None, None, :] == slot_ids[None, :, None])
    )
    routing = routing.astype(jnp.bfloat16)
    packed = jnp.einsum(
        "oks,srd->kord", routing, arrived, preferred_element_type=jnp.float32
    ).astype(jnp.bfloat16)
    packed = packed.reshape(slot_count, groups * piece_rows, block_width)
    blocks = lax.all_to_all(packed, "grp", split_axis=1, concat_axis=1, tiled=True)
    left_product = jnp.einsum(
        "kab,kbc->kac", left_factor, blocks, preferred_element_type=jnp.float32
    ).astype(jnp.bfloat16)
    result = jnp.einsum(
        "kab,kbc->kac", left_product, right_factor, preferred_element_type=jnp.float32
    ).astype(jnp.bfloat16)
    returned = lax.all_to_all(result, "grp", split_axis=1, concat_axis=1, tiled=True)
    returned = returned.reshape(slot_count, groups, piece_rows, block_width)
    unpacked = jnp.einsum(
        "oks,kord->srd", routing, returned, preferred_element_type=jnp.float32
    ).astype(jnp.bfloat16)
    homeward = lax.all_to_all(
        unpacked.reshape(columns * piece_rows, block_width),
        "fsdp",
        split_axis=0,
        concat_axis=0,
        tiled=True,
    )
    homeward = homeward.reshape(columns, piece_rows, block_width)
    return jnp.einsum(
        "cj,crd->jrd", pick_send, homeward, preferred_element_type=jnp.float32
    ).astype(jnp.bfloat16)


def solution(mesh):
    return jax.shard_map(
        per_device,
        mesh=mesh,
        in_specs=(
            P("fsdp", "grp", None),
            P(("fsdp", "grp"), None, None),
            P(("fsdp", "grp"), None, None),
            P(),
        ),
        out_specs=P("fsdp", "grp", None),
        check_vma=False,
    )
```

profile of v0, /device:TPU:0, one launch (start us, length us, event | category | flops | bytes accessed | tf_op | source)
XLA Modules:
  0.0 135.2 jit_solution(5954696607277778726)
XLA Ops:
  0.0 0.0 copy-start
  0.0 0.8 reshape.94
  0.9 1.6 %convolution_convert_fusion.3 = bf16[8,128,512]{2,0,1:T(8,128)(2,1)S(1)} fusion(bf16[3,128,512]{2,1,0:T(8,128)(2,1)} %param.4, s32[3]{0:T(128)S(1)} %dynamic-slice_bitcast_fusion), kind=kOutput, calls=%fused_computation.7 | convolution fusion | flops 3670040 | bytes 1441804 | tf_op jit(solution)/shard_map/cj,jrd->crd/dot_general | solution.py:22
  2.5 1.3 copy.33
  3.8 7.3 %all-to-all-start = ((bf16[8,128,512]{2,1,0:T(8,128)(2,1)}), bf16[8,128,512]{2,1,0:T(8,128)(2,1)S(1)}, u32[]{:S(2)}, u32[]{:S(2)}) async-start(bf16[8,128,512]{2,1,0:T(8,128)(2,1)} %copy.33), calls=%async_computation | async-start | bytes 2097152 | tf_op jit(solution)/shard_map/all_to_all | solution.py:25
  11.1 0.1 convert_reduce_fusion.1
  11.2 0.2 convert_reduce_fusion
  11.4 25.4 %all-to-all-done = bf16[8,128,512]{2,1,0:T(8,128)(2,1)S(1)} async-done(((bf16[8,128,512]{2,1,0:T(8,128)(2,1)}), bf16[8,128,512]{2,1,0:T(8,128)(2,1)S(1)}, u32[]{:S(2)}, u32[]{:S(2)}) %all-to-all-start) | async-done | bytes 1048608 | tf_op jit(solution)/shard_map/all_to_all | solution.py:25
  36.8 1.0 fusion.2
  37.9 0.3 copy.35
  38.2 1.4 copy.36
  39.6 28.9 %all_to_all.22 = bf16[3,512,512]{2,0,1:T(4,128)(2,1)} all-to-all(bf16[3,512,512]{2,0,1:T(4,128)(2,1)S(1)} %copy.36), channel_id=1, replica_groups=mesh['fsdp'=8,'grp'=4] {'grp'}, dimensions={1} | all-to-all | bytes 3145728 | tf_op jit(solution)/shard_map/all_to_all | solution.py:51
  68.5 0.0 copy-done
  68.5 4.2 %convolution_convert_fusion = bf16[3,512,512]{2,1,0:T(8,128)(2,1)S(1)} fusion(bf16[3,512,512]{2,1,0:T(8,128)(2,1)S(1)} %copy-done, bf16[3,512,512]{2,1,0:T(8,128)(2,1)} %param.5, bf16[3,512,512]{2,0,1:T(4,128)(2,1)} %all_to_all.22), kind=kOutput, calls=%fused_computation.1 | convolution fusion | flops 1612185600 | bytes 6291456 | tf_op jit(solution)/shard_map/kab,kbc->kac/dot_general | solution.py:55
  72.7 1.4 copy.39
  74.0 28.1 %all_to_all.23 = bf16[3,512,512]{2,0,1:T(4,128)(2,1)S(1)} all-to-all(bf16[3,512,512]{2,0,1:T(4,128)(2,1)S(1)} %copy.39), channel_id=1, replica_groups=mesh['fsdp'=8,'grp'=4] {'grp'}, dimensions={1} | all-to-all | bytes 3145728 | tf_op jit(solution)/shard_map/all_to_all | solution.py:58
  102.2 2.2 %bitcast_convert_fusion = bf16[8,128,512]{2,0,1:T(8,128)(2,1)S(1)} fusion(bf16[3,4,128,512]{3,0,2,1:T(4,128)(2,1)S(1)} %bitcast.23, pred[3,8]{1,0:T(4,128)(4,1)S(1)} %iota_compare_fusion.1, pred[4,8]{1,0:T(4,128)(4,1)S(1)} %fusion.22), kind=kOutput, calls=%fused_computation | convolution fusion | flops 13107296 | bytes 2621496 | tf_op jit(solution)/shard_map/oks,kord->srd/dot_general | solution.py:60
  104.4 0.3 copy.42
  104.7 28.8 %all_to_all.24 = bf16[8,128,512]{2,1,0:T(8,128)(2,1)S(1)} all-to-all(bf16[8,128,512]{2,1,0:T(8,128)(2,1)S(1)} %copy.42), channel_id=1, replica_groups=mesh['fsdp'=8,'grp'=4] {'fsdp'}, dimensions={0} | all-to-all | bytes 2097152 | tf_op jit(solution)/shard_map/all_to_all | solution.py:63
  133.6 0.8 convolution_convert_fusion.4
  134.4 0.8 copy.44
  (5 shorter events, 0.0 us)
Async XLA Ops:
  0.0 68.5 %copy-start = (bf16[3,512,512]{2,1,0:T(8,128)(2,1)S(1)}, bf16[3,512,512]{2,1,0:T(8,128)(2,1)}, u32[]{:S(2)}) copy-start(bf16[3,512,512]{2,1,0:T(8,128)(2,1)} %param.6) | copy-start | bytes 4718596
  3.8 33.0 %all-to-all-start = ((bf16[8,128,512]{2,1,0:T(8,128)(2,1)}), bf16[8,128,512]{2,1,0:T(8,128)(2,1)S(1)}, u32[]{:S(2)}, u32[]{:S(2)}) async-start(bf16[8,128,512]{2,1,0:T(8,128)(2,1)} %copy.33), calls=%async_computation | async-start | bytes 2097152 | tf_op jit(solution)/shard_map/all_to_all | solution.py:25
where the time goes:
time: 136 us; the launch traced here: 135 us
  blocking collectives  85.9 us (63%)
  waiting for transfers between devices  25.4 us (19%)
  matrix products  9.85 us (7%)
  starting transfers between devices  7.28 us (5%)
  local copies, waits for them, and re-layouts  6.34 us (5%)
    all_to_all x1, blocking collectives, per_device(): lax.all_to_all(packed, 'grp', split_axis=1, concat_axis=1, tiled=True)  28.9 us
    all_to_all x1, blocking collectives, per_device(): lax.all_to_all(unpacked.reshape(columns * piece_rows, block_width), 'fsdp...  28.8 us
    all_to_all x1, blocking collectives, per_device(): lax.all_to_all(result, 'grp', split_axis=1, concat_axis=1, tiled=True)  28.1 us
    all_to_all x1, waiting for transfers between devices, per_device(): lax.all_to_all(outgoing.reshape(columns * piece_rows, block_width), 'fsdp...  25.4 us
    all_to_all x1, starting transfers between devices, per_device(): lax.all_to_all(outgoing.reshape(columns * piece_rows, block_width), 'fsdp...  7.28 us
    dot_general x1, matrix products, per_device(): jnp.einsum('kab,kbc->kac', left_product, right_factor, preferred_element_...  4.21 us
  transfers between devices with their start and end apart: 1, of which 1 were waited for; matrix products, arithmetic and copies ran while one was open for 0% of the time, Pallas kernels for 0%

commit v1 on v0

--- a/solution.py
+++ b/solution.py
@@ -48,7 +48,10 @@
         "oks,srd->kord", routing, arrived, preferred_element_type=jnp.float32
     ).astype(jnp.bfloat16)
     packed = packed.reshape(slot_count, groups * piece_rows, block_width)
-    blocks = lax.all_to_all(packed, "grp", split_axis=1, concat_axis=1, tiled=True)
+    blocks = jnp.concatenate(
+        lax.all_to_all(jnp.stack(jnp.split(packed, lax.axis_size("grp"), axis=1)), "grp", 0, 0),
+        axis=1,
+    )
     left_product = jnp.einsum(
         "kab,kbc->kac", left_factor, blocks, preferred_element_type=jnp.float32
     ).astype(jnp.bfloat16)

time: 136 us -> 129 us (0.949)
  blocking collectives: 85.9 us -> 79.6 us
    all_to_all x1, blocking collectives: 28.9 us -> 22.6 us  [per_device(): lax.all_to_all(jnp.stack(jnp.split(packed, lax.axis_size('grp'), axis=1))...]
where the time goes in v1:
time: 129 us
  blocking collectives  79.6 us (62%)
  waiting for transfers between devices  25.4 us (20%)
  matrix products  9.51 us (7%)
  starting transfers between devices  7.28 us (6%)
  local copies, waits for them, and re-layouts  6.35 us (5%)
    all_to_all x1, blocking collectives, per_device(): lax.all_to_all(unpacked.reshape(columns * piece_rows, block_width), 'fsdp...  28.8 us
    all_to_all x1, blocking collectives, per_device(): lax.all_to_all(result, 'grp', split_axis=1, concat_axis=1, tiled=True)  28.1 us
    all_to_all x1, waiting for transfers between devices, per_device(): lax.all_to_all(outgoing.reshape(columns * piece_rows, block_width), 'fsdp...  25.4 us
    all_to_all x1, blocking collectives, per_device(): lax.all_to_all(jnp.stack(jnp.split(packed, lax.axis_size('grp'), axis=1))...  22.6 us
    all_to_all x1, starting transfers between devices, per_device(): lax.all_to_all(outgoing.reshape(columns * piece_rows, block_width), 'fsdp...  7.28 us
    dot_general x1, matrix products, per_device(): jnp.einsum('kab,kbc->kac', left_product, right_factor, preferred_element_...  3.87 us
  transfers between devices with their start and end apart: 1, of which 1 were waited for; matrix products, arithmetic and copies ran while one was open for 0% of the time, Pallas kernels for 0%

profile of v1, /device:TPU:0, one launch (start us, length us, event | category | flops | bytes accessed | tf_op | source)
XLA Modules:
  0.0 128.8 jit_solution(16596608995751139249)
XLA Ops:
  0.0 0.0 copy-start
  0.0 0.8 reshape.100
  0.9 1.6 %convolution_convert_fusion.3 = bf16[8,128,512]{2,0,1:T(8,128)(2,1)S(1)} fusion(bf16[3,128,512]{2,1,0:T(8,128)(2,1)} %param.4, s32[3]{0:T(128)S(1)} %dynamic-slice_bitcast_fusion), kind=kOutput, calls=%fused_computation.7 | convolution fusion | flops 3670040 | bytes 1441804 | tf_op jit(solution)/shard_map/cj,jrd->crd/dot_general | solution.py:22
  2.5 1.3 %copy.34 = bf16[8,128,512]{2,1,0:T(8,128)(2,1)} copy(bf16[8,128,512]{2,0,1:T(8,128)(2,1)S(1)} %convolution_convert_fusion.3) | data formatting | bytes 2097152 | tf_op jit(solution)/shard_map/convert_element_type | solution.py:24
  3.8 7.3 %all-to-all-start = ((bf16[8,128,512]{2,1,0:T(8,128)(2,1)}), bf16[8,128,512]{2,1,0:T(8,128)(2,1)S(1)}, u32[]{:S(2)}, u32[]{:S(2)}) async-start(bf16[8,128,512]{2,1,0:T(8,128)(2,1)} %copy.34), calls=%async_computation | async-start | bytes 2097152 | tf_op jit(solution)/shard_map/all_to_all | solution.py:25
  11.1 0.1 convert_reduce_fusion.1
  11.2 0.2 convert_reduce_fusion
  11.4 25.4 %all-to-all-done = bf16[8,128,512]{2,1,0:T(8,128)(2,1)S(1)} async-done(((bf16[8,128,512]{2,1,0:T(8,128)(2,1)}), bf16[8,128,512]{2,1,0:T(8,128)(2,1)S(1)}, u32[]{:S(2)}, u32[]{:S(2)}) %all-to-all-start) | async-done | bytes 1048608 | tf_op jit(solution)/shard_map/all_to_all | solution.py:25
  36.8 1.0 fusion.1
  37.9 0.3 copy.36
  38.2 0.1 slice_bitcast_fusion.3
  38.3 0.2 pad_maximum_fusion
  38.5 22.6 %all_to_all.22 = bf16[4,3,128,512]{3,2,1,0:T(8,128)(2,1)S(1)} all-to-all(bf16[4,3,128,512]{3,2,1,0:T(8,128)(2,1)S(1)} %pad_maximum_fusion), channel_id=1, replica_groups=mesh['fsdp'=8,'grp'=4] {'grp'}, dimensions={0} | all-to-all | bytes 3145728 | tf_op jit(solution)/shard_map/all_to_all | solution.py:52
  61.2 1.3 copy.37
  62.4 0.0 copy-done
  62.4 3.9 %convolution_convert_fusion = bf16[3,512,512]{2,1,0:T(8,128)(2,1)S(1)} fusion(bf16[3,512,512]{2,1,0:T(8,128)(2,1)S(1)} %copy-done, bf16[3,512,512]{2,1,0:T(8,128)(2,1)} %bitcast.36, bf16[3,512,512]{2,1,0:T(8,128)(2,1)} %param.5), kind=kOutput, calls=%fused_computation.1 | convolution fusion | flops 1612185600 | bytes 6291456 | tf_op jit(solution)/shard_map/kab,kbc->kac/dot_general | solution.py:58
  66.3 1.4 %copy.40 = bf16[3,512,512]{2,0,1:T(4,128)(2,1)S(1)} copy(bf16[3,512,512]{2,1,0:T(8,128)(2,1)S(1)} %convolution_convert_fusion) | data formatting | bytes 3145728 | tf_op jit(solution)/shard_map/convert_element_type | solution.py:60
  67.7 28.1 %all_to_all.23 = bf16[3,512,512]{2,0,1:T(4,128)(2,1)S(1)} all-to-all(bf16[3,512,512]{2,0,1:T(4,128)(2,1)S(1)} %copy.40), channel_id=1, replica_groups=mesh['fsdp'=8,'grp'=4] {'grp'}, dimensions={1} | all-to-all | bytes 3145728 | tf_op jit(solution)/shard_map/all_to_all | solution.py:61
  95.8 2.2 %bitcast_convert_fusion = bf16[8,128,512]{2,0,1:T(8,128)(2,1)S(1)} fusion(bf16[3,4,128,512]{3,0,2,1:T(4,128)(2,1)S(1)} %bitcast.35, pred[3,8]{1,0:T(4,128)(4,1)S(1)} %iota_compare_fusion.1, pred[4,8]{1,0:T(4,128)(4,1)S(1)} %fusion.19), kind=kOutput, calls=%fused_computation | convolution fusion | flops 13107296 | bytes 2621496 | tf_op jit(solution)/shard_map/oks,kord->srd/dot_general | solution.py:63
  98.0 0.3 copy.43
  98.4 28.8 %all_to_all.24 = bf16[8,128,512]{2,1,0:T(8,128)(2,1)S(1)} all-to-all(bf16[8,128,512]{2,1,0:T(8,128)(2,1)S(1)} %copy.43), channel_id=1, replica_groups=mesh['fsdp'=8,'grp'=4] {'fsdp'}, dimensions={0} | all-to-all | bytes 2097152 | tf_op jit(solution)/shard_map/all_to_all | solution.py:66
  127.2 0.8 convolution_convert_fusion.4
  128.0 0.8 copy.45
  (5 shorter events, 0.0 us)
Async XLA Ops:
  0.0 62.4 %copy-start = (bf16[3,512,512]{2,1,0:T(8,128)(2,1)S(1)}, bf16[3,512,512]{2,1,0:T(8,128)(2,1)}, u32[]{:S(2)}) copy-start(bf16[3,512,512]{2,1,0:T(8,128)(2,1)} %param.6) | copy-start | bytes 4718596
  3.8 33.0 %all-to-all-start = ((bf16[8,128,512]{2,1,0:T(8,128)(2,1)}), bf16[8,128,512]{2,1,0:T(8,128)(2,1)S(1)}, u32[]{:S(2)}, u32[]{:S(2)}) async-start(bf16[8,128,512]{2,1,0:T(8,128)(2,1)} %copy.34), calls=%async_computation | async-start | bytes 2097152 | tf_op jit(solution)/shard_map/all_to_all | solution.py:25
